TPU v7x, 32 devices: a whole 2x2x4 slice. The times are simulated.
32 devices in a mesh: member: 2 (over x), lat: 16 (over z, y, core).
Axes of the slice: x: 2, y: 2, z: 4, core: 2. Of those that a mesh axis runs over, the one named last changes fastest.
Arguments:
- height: float32 [128, 32, 1440], P(('member', 'lat')), parts along dimension 0, may hold values from -6 to 6
- zonal_courant: float32 [128, 32, 1440], P(('member', 'lat')), parts along dimension 0, may hold values from -1.5 to 1.5
- merid_courant: float32 [128, 32, 1440], P(('member', 'lat')), parts along dimension 0, may hold values from -1.5 to 1.5
- rates: float32 [64], P('member'), parts along dimension 0, may hold values from 0.05 to 0.5
- thresholds: float32 [64], P('member'), parts along dimension 0, may hold values from -3 to 3
- flags: int32 [64], replicated, may hold values from 0 to 1, as said below
- cutoffs: int32 [64], replicated, may hold values from 45 to 360
Outputs:
- filtered_height: float32 [128, 32, 1440], P(('member', 'lat')), parts along dimension 0
There are 2 independent parts, one for each index of `member`. A program takes and returns all parts, laid end to end along the dimension named above; an argument that names none is the same for every part. Nothing has to cross between parts.
Inputs may be any that keep to these rules, and one draw needn't show every extreme that they name: flags is 1 on a southern band of rows that starts at row 0 and on a northern band that ends at row 63, each band 64 // 8 to 16 rows long, and 0 on all other rows.
All inputs are finite; a program needn't handle non-finite values.
Results may differ from a plain program's by a relative error of at most 0.00007.
Values sent between devices are 32-bit elements; how exact they have to be, the bound alone decides.
No kernel may reach another device: no remote copies, remote signals or barrier semaphores. Data moves between devices by JAX's collectives and lax.ppermute only.
A program may use at most 64 MiB of HBM per device.

v0:
```python
import jax
import jax.numpy as jnp
from jax import lax
from jax.sharding import PartitionSpec as P


def padded_2(cells, sides, width):
    for axis, dim in sides:
        count = lax.axis_size(axis)
        ends = count - 1
        head = lax.slice_in_dim(cells, 0, width, axis=dim)
        tail = lax.slice_in_dim(cells, cells.shape[dim] - width, cells.shape[dim], axis=dim)
        cells = jnp.concatenate(
            [
                lax.ppermute(tail, axis, [(i, (i + 1) % count) for i in range(ends)]),
                cells,
                lax.ppermute(head, axis, [((i + 1) % count, i) for i in range(ends)]),
            ],
            axis=dim,
        )
    return cells


def transform_table(nlon, nkp):
    points = jnp.arange(nlon, dtype=jnp.int32)
    waves = jnp.arange(nkp, dtype=jnp.int32)
    phase = points[:, None] * waves[None, :] % nlon
    angle = 2.0 * jnp.pi / nlon * phase.astype(jnp.float32)
    return jnp.concatenate([jnp.cos(angle), jnp.sin(angle)], axis=1)


def wave_weights(nlon, nkp):
    waves = jnp.arange(nkp, dtype=jnp.int32)
    interior = jnp.where((waves > 0) & (waves < nlon // 2), 2.0, 1.0)
    return jnp.where(waves <= nlon // 2, interior, 0.0).astype(jnp.float32) / nlon


def damping(row_flags, row_cutoffs, nkp):
    waves = jnp.maximum(jnp.arange(nkp), 1).astype(jnp.float32)
    ratio = row_cutoffs.astype(jnp.float32)[:, None] / waves[None, :]
    factor = jnp.minimum(1.0, ratio * ratio)
    return jnp.where(row_flags[:, None] > 0, factor, 1.0)


def filter_units(flat, damp, table, weights):
    highest = lax.Precision.HIGHEST
    spectrum = jnp.dot(flat, table, precision=highest, preferred_element_type=jnp.float32)
    factor = (1.0 - damp) * weights[None, :]
    scaled = spectrum * jnp.concatenate([factor, factor], axis=1)
    dims = (((1,), (1,)), ((), ()))
    removed = lax.dot_general(
        scaled, table, dims, precision=highest, preferred_element_type=jnp.float32
    )
    return flat - removed


def filtered_or_kept(block, row_flags, row_cutoffs, table, weights):
    rows, levels, nlon = block.shape
    damp = damping(row_flags, row_cutoffs, weights.shape[0])
    unit_damp = jnp.broadcast_to(damp[:, None, :], (rows, levels, damp.shape[1])).reshape(
        rows * levels, damp.shape[1]
    )

    def apply_filter(data):
        return filter_units(data.reshape(rows * levels, nlon), unit_damp, table, weights).reshape(
            rows, levels, nlon
        )

    def keep_block(data):
        return data

    return lax.cond(jnp.any(row_flags > 0), apply_filter, keep_block, block)


def face_fluxes(rows_height, rows_speed, face_cos, count):
    face_value = (
        7.0 * (rows_height[1 : count + 1] + rows_height[2 : count + 2])
        - (rows_height[0:count] + rows_height[3 : count + 3])
    ) / 12.0
    speed = 0.5 * (rows_speed[0:count] + rows_speed[1 : count + 1]) * face_cos[:, None, None]
    return speed * face_value


def face_cosines(face_ids, nlat):
    return jnp.where(
        (face_ids > 0) & (face_ids < nlat),
        jnp.sin(jnp.pi * face_ids.astype(jnp.float32) / nlat),
        jnp.float32(0.0),
    )


def local(height, zonal_courant, merid_courant, rates, thresholds, flags, cutoffs):
    lat_rows, levels, nlon = height.shape
    devices = lax.axis_size("lat")
    position = lax.axis_index("lat")
    first_row = position * lat_rows
    nlat = lat_rows * devices
    local_rows = first_row + jnp.arange(lat_rows, dtype=jnp.int32)
    cos_rows = jnp.sin(jnp.pi * (local_rows.astype(jnp.float32) + 0.5) / nlat)
    faces = first_row + jnp.arange(lat_rows + 1, dtype=jnp.int32)
    cos_faces = face_cosines(faces, nlat)
    padded = padded_2(jnp.stack([height, merid_courant]), (("lat", 1),), 2)
    east = jnp.roll(height, -1, axis=2)
    west = jnp.roll(height, 1, axis=2)
    far_east = jnp.roll(height, -2, axis=2)
    face_height = (7.0 * (height + east) - (west + far_east)) / 12.0
    face_speed = 0.5 * (zonal_courant + jnp.roll(zonal_courant, -1, axis=2))
    zonal_flux = face_speed * face_height
    zonal_div = zonal_flux - jnp.roll(zonal_flux, 1, axis=2)
    source = -rates[None, :, None] * jax.nn.softplus(height - thresholds[None, :, None])
    partial_sums = jnp.sum(jnp.sum(source, axis=2) * cos_rows[:, None], axis=0)
    totals = lax.psum(partial_sums, "lat")
    all_rows = jnp.arange(nlat, dtype=jnp.int32)
    area = nlon * jnp.sum(jnp.sin(jnp.pi * (all_rows.astype(jnp.float32) + 0.5) / nlat))
    level_mean = totals / area
    padded_height = padded[0]
    padded_speed = padded[1]
    count = lat_rows + 1
    merid_flux = face_fluxes(padded_height, padded_speed[1:], cos_faces, count)
    merid_div = (merid_flux[1:] - merid_flux[:-1]) / cos_rows[:, None, None]
    updated = height - zonal_div - merid_div + source - level_mean[None, :, None]
    nkp = (nlon // 2 + 128) // 128 * 128
    table = transform_table(nlon, nkp)
    weights = wave_weights(nlon, nkp)
    row_flags = lax.dynamic_slice_in_dim(flags, first_row, lat_rows)
    row_cutoffs = lax.dynamic_slice_in_dim(cutoffs, first_row, lat_rows)
    result = filtered_or_kept(updated, row_flags, row_cutoffs, table, weights)
    return result


def solution(mesh):
    return jax.shard_map(
        local,
        mesh=mesh,
        in_specs=(
            P(("member", "lat"), None, None),
            P(("member", "lat"), None, None),
            P(("member", "lat"), None, None),
            P("member"),
            P("member"),
            P(),
            P(),
        ),
        out_specs=P(("member", "lat"), None, None),
        check_vma=False,
    )
```

profile of v0, /device:TPU:0, one launch (start us, length us, event | category | flops | bytes accessed | tf_op | source)
XLA Modules:
  0.0 101.5 jit_solution(3019089762479028692)
XLA Ops:
  0.0 0.0 copy-start
  0.0 0.0 copy-start.2
  0.0 2.8 %fusion.17 = (f32[2,2,32,1440]{3,2,1,0:T(8,128)}, f32[2,2,32,1440]{3,2,1,0:T(8,128)}) fusion(f32[1,4,32,1440]{3,2,1,0:T(8,128)} %bitcast.21, f32[1,4,32,1440]{3,2,1,0:T(8,128)} %bitcast.27), kind=kLoop, calls=%fused_computation.33 | loop fusion | flops 368640 | bytes 2949120 | tf_op jit(solution)/shard_map/stack | solution.py:102
  2.8 3.3 %collective-permute-start = (f32[2,2,32,1440]{3,2,1,0:T(8,128)}, f32[2,2,32,1440]{3,2,1,0:T(8,128)}, u32[]{:S(2)}, u32[]{:S(2)}) collective-permute-start(f32[2,2,32,1440]{3,2,1,0:T(8,128)} %get-tuple-element.115), channel_id=1, source_target_pairs={{0,1},{1,2},{2,3},{3,4},{4,5},{5,6},{6,7},{7,8},{8,9},{9,10},{10,1... | collective-permute-start | bytes 2211848 | tf_op jit(solution)/shard_map/ppermute | solution.py:15
  6.1 1.3 %collective-permute-start.1 = (f32[2,2,32,1440]{3,2,1,0:T(8,128)}, f32[2,2,32,1440]{3,2,1,0:T(8,128)}, u32[]{:S(2)}, u32[]{:S(2)}) collective-permute-start(f32[2,2,32,1440]{3,2,1,0:T(8,128)} %get-tuple-element.116), channel_id=1, source_target_pairs={{1,0},{2,1},{3,2},{4,3},{5,4},{6,5},{7,6},{8,7},{9,8},{10,9},{11,1... | collective-permute-start | bytes 2211848 | tf_op jit(solution)/shard_map/ppermute | solution.py:17
  7.3 2.8 %fusion.33 = (f32[4,32,1439]{2,1,0:T(8,128)}, f32[4,32,1439]{2,1,0:T(8,128)}) fusion(f32[4,32,1440]{2,1,0:T(8,128)} %param.9), kind=kLoop, calls=%fused_computation.63 | loop fusion | bytes 2947072 | tf_op jit(solution)/shard_map/jit(_roll_static)/slice | solution.py:104
  10.1 0.0 copy-done
  10.1 0.1 fusion.32
  10.2 0.3 slice.95
  10.5 0.0 copy-done.2
  10.5 1.2 %slice.89 = f32[4,32,1439]{2,1,0:T(8,128)} slice(f32[4,32,1440]{2,1,0:T(8,128)S(1)} %copy-done.2), slice={[0:4], [0:32], [1:1440]} | slice | bytes 1473536 | tf_op jit(solution)/shard_map/jit(_roll_static)/slice | solution.py:107
  11.8 0.7 sine_reduce_fusion
  12.4 0.0 copy-start.9
  12.4 0.0 slice-start
  12.4 0.0 copy-start.3
  12.4 0.0 copy-start.4
  12.4 0.0 copy-start.5
  12.4 0.0 copy-start.7
  12.5 19.6 %fusion.7 = (f32[1440,768]{1,0:T(8,128)}, f32[1440,768]{1,0:T(8,128)}) fusion(), kind=kLoop, calls=%fused_computation.15 | loop fusion | flops 9953280 | bytes 8847360 | tf_op jit(solution)/shard_map/sin | solution.py:29
  32.0 0.0 copy-start.8
  32.0 0.0 copy-start.10
  32.0 0.0 copy-done.9
  32.1 0.0 slice-done
  32.1 0.0 copy-done.3
  32.1 0.0 copy-done.4
  32.1 0.0 copy-done.5
  32.1 0.0 copy-done.7
  32.1 0.9 fusion.29
  33.0 0.1 multiply_reduce_fusion
  33.1 35.8 %psum.7 = f32[32]{0:T(128)S(1)} all-reduce(f32[32]{0:T(128)S(1)} %multiply_reduce_fusion), channel_id=1, replica_groups=mesh['member'=2,'lat'=16] {'lat'}, use_global_device_ids=true, to_apply=%region_3.4 | all-reduce | flops 32 | bytes 256 | tf_op jit(solution)/shard_map/psum | solution.py:112
  68.9 0.1 slice.109
  69.0 0.0 copy-done.8
  69.0 0.8 fusion.31
  69.8 0.0 copy-done.10
  69.8 0.1 dynamic-slice_convert_fusion
  71.2 0.0 copy-start.6
  71.2 8.2 %pad_maximum_fusion = f32[1440,1536]{1,0:T(8,128)} fusion(f32[1440,768]{1,0:T(8,128)} %get-tuple-element.123, f32[1440,768]{1,0:T(8,128)} %get-tuple-element.124), kind=kLoop, calls=%fused_computation.8 | loop fusion | flops 2211840 | bytes 17694720 | tf_op jit(solution)/shard_map/concatenate | solution.py:29
  79.4 0.0 collective-permute-done
  79.4 0.0 collective-permute-done.1
  79.4 0.0 copy-done.6
  79.4 1.9 %maximum_maximum_fusion = (f32[2,6,32,1440]{3,2,1,0:T(8,128)S(1)}, f32[2,6,32,1440]{3,2,1,0:T(8,128)S(1)}) fusion(f32[1,4,32,1440]{3,2,1,0:T(8,128)S(1)} %bitcast.28, f32[1,4,32,1440]{3,2,1,0:T(8,128)S(1)} %bitcast.22, f32[2,2,32,1440]{3,2,1,0:T(8,128)} %collective-permute-done, f32[2,2,32,1440]{3,2,1,0:T(8,128)} %collective-permute-done.1), kind=kLoop, calls=%fused_computation.18 | loop fusion | flops 2211840 | bytes 7372800 | tf_op jit(solution)/shard_map/concatenate | solution.py:13
  81.3 0.5 fusion.13
  81.8 0.7 fusion.22
  82.6 18.0 %conditional.1 = (f32[4,32,1440]{2,1,0:T(8,128)S(1)}) conditional(s32[]{:T(128)} %convert_element_type.42, f32[4,32,1440]{2,1,0:T(8,128)S(1)} %fusion.22, (f32[4,32,1440]{2,1,0:T(8,128)S(1)}, f32[1440,1536]{1,0:T(8,128)}, pred[4]{0:T(512)(128)(4,1)S(1)}, f32[4]{0:T(128)S(1)}, f32[1,768]{1,0:T(1,128)S(1)}, /*index=5*/s32[768]{0:T(1024)S(1)}) %tuple.45), branch_computations={%region_5.6_spmd, %region_6.7_spmd} | conditional | flops 6795468800 | bytes 25258016 | solution.py:72
  82.8 0.1 fusion.2
  82.9 7.6 %convolution_multiply_fusion = f32[128,1536]{1,0:T(8,128)S(1)} fusion(f32[128,1440]{1,0:T(8,128)S(1)} %bitcast.24, f32[1440,1536]{1,0:T(8,128)} %get-tuple-element.105, f32[128,768]{1,0:T(8,128)S(1)} %bitcast_multiply_fusion), kind=kOutput, calls=%fused_computation.1 | convolution fusion | flops 3397779456 | bytes 10764288 | tf_op jit(solution)/shard_map/cond/branch_1_fun/dot_general | solution.py:47
  90.6 0.3 copy.27
  90.8 9.5 %convolution_subtract_fusion = f32[128,1440]{0,1:T(8,128)S(1)} fusion(f32[128,1440]{0,1:T(8,128)S(1)} %copy.27, f32[128,1536]{1,0:T(8,128)S(1)} %convolution_multiply_fusion, f32[1440,1536]{1,0:T(8,128)} %get-tuple-element.105), kind=kOutput, calls=%fused_computation | convolution fusion | flops 3397570560 | bytes 11108352 | tf_op jit(solution)/shard_map/cond/branch_1_fun/dot_general | solution.py:51
  100.3 0.3 copy.28
  100.6 0.0 copy-start.1
  100.6 0.9 copy-done.1
  (10 shorter events, 0.2 us)
Async XLA Ops:
  0.0 10.1 %copy-start = (f32[4,32,1440]{2,1,0:T(8,128)S(1)}, f32[4,32,1440]{2,1,0:T(8,128)}, u32[]{:S(2)}) copy-start(f32[4,32,1440]{2,1,0:T(8,128)} %param.9) | copy-start | bytes 2211844
  0.0 10.5 %copy-start.2 = (f32[4,32,1440]{2,1,0:T(8,128)S(1)}, f32[4,32,1440]{2,1,0:T(8,128)}, u32[]{:S(2)}) copy-start(f32[4,32,1440]{2,1,0:T(8,128)} %param.10) | copy-start | bytes 2211844
  2.8 76.6 %collective-permute-start = (f32[2,2,32,1440]{3,2,1,0:T(8,128)}, f32[2,2,32,1440]{3,2,1,0:T(8,128)}, u32[]{:S(2)}, u32[]{:S(2)}) collective-permute-start(f32[2,2,32,1440]{3,2,1,0:T(8,128)} %get-tuple-element.115), channel_id=1, source_target_pairs={{0,1},{1,2},{2,3},{3,4},{4,5},{5,6},{6,7},{7,8},{8,9},{9,10},{10,1... | collective-permute-start | bytes 2211848 | tf_op jit(solution)/shard_map/ppermute | solution.py:15
  6.1 73.3 %collective-permute-start.1 = (f32[2,2,32,1440]{3,2,1,0:T(8,128)}, f32[2,2,32,1440]{3,2,1,0:T(8,128)}, u32[]{:S(2)}, u32[]{:S(2)}) collective-permute-start(f32[2,2,32,1440]{3,2,1,0:T(8,128)} %get-tuple-element.116), channel_id=1, source_target_pairs={{1,0},{2,1},{3,2},{4,3},{5,4},{6,5},{7,6},{8,7},{9,8},{10,9},{11,1... | collective-permute-start | bytes 2211848 | tf_op jit(solution)/shard_map/ppermute | solution.py:17
  12.4 19.6 %copy-start.9 = (f32[32]{0:T(128)S(1)}, f32[32]{0:T(128)}, u32[]{:S(2)}) copy-start(f32[32]{0:T(128)} %param.12) | copy-start | bytes 388
  12.4 19.6 %slice-start = ((f32[4,32,1440]{2,1,0:T(8,128)}), f32[4,32,1]{2,1,0:T(8,128)S(1)}, s32[]{:S(2)}) async-start(f32[4,32,1440]{2,1,0:T(8,128)} %param.10), calls=%async_computation | async-start | bytes 131072 | tf_op jit(solution)/shard_map/jit(_roll_static)/slice | solution.py:107
  12.4 19.7 %copy-start.3 = (f32[4,32,1439]{2,1,0:T(8,128)S(1)}, f32[4,32,1439]{2,1,0:T(8,128)}, u32[]{:S(2)}) copy-start(f32[4,32,1439]{2,1,0:T(8,128)} %slice.89) | copy-start | bytes 2210308
  12.4 19.7 %copy-start.4 = (f32[4,32,1439]{2,1,0:T(8,128)S(1)}, f32[4,32,1439]{2,1,0:T(8,128)}, u32[]{:S(2)}) copy-start(f32[4,32,1439]{2,1,0:T(8,128)} %get-tuple-element.121) | copy-start | bytes 2210308
  12.4 19.7 %copy-start.5 = (f32[4,32,1439]{2,1,0:T(8,128)S(1)}, f32[4,32,1439]{2,1,0:T(8,128)}, u32[]{:S(2)}) copy-start(f32[4,32,1439]{2,1,0:T(8,128)} %get-tuple-element.122) | copy-start | bytes 2210308
  12.4 19.7 %copy-start.7 = (f32[32]{0:T(128)S(1)}, f32[32]{0:T(128)}, u32[]{:S(2)}) copy-start(f32[32]{0:T(128)} %param.13) | copy-start | bytes 388
  32.0 37.0 %copy-start.8 = (s32[64]{0:T(128)S(1)}, s32[64]{0:T(128)}, u32[]{:S(2)}) copy-start(s32[64]{0:T(128)} %param.14) | copy-start | bytes 772
  32.0 37.8 %copy-start.10 = (s32[64]{0:T(128)S(1)}, s32[64]{0:T(128)}, u32[]{:S(2)}) copy-start(s32[64]{0:T(128)} %param.15) | copy-start | bytes 772
  71.2 8.2 %copy-start.6 = (f32[4,32,1440]{2,1,0:T(8,128)S(1)}, f32[4,32,1440]{2,1,0:T(8,128)}, u32[]{:S(2)}) copy-start(f32[4,32,1440]{2,1,0:T(8,128)} %param.11) | copy-start | bytes 2211844
  100.6 0.9 copy-start.1
where the time goes:
time: 102 us; the launch traced here: 101 us
  other arithmetic  36.4 us (36%)
  blocking collectives  35.8 us (35%)
  matrix products  17.1 us (17%)
  local copies, waits for them, and re-layouts  5.82 us (6%)
  starting transfers between devices  4.55 us (4%)
  between operations  1.52 us (1%)
    psum x1, blocking collectives, local(): totals = lax.psum(partial_sums, 'lat')  35.8 us
    sin x1, other arithmetic, transform_table(): return jnp.concatenate([jnp.cos(angle), jnp.sin(angle)], axis=1)  19.6 us
    dot_general x1, matrix products, filter_units(): lax.dot_general(scaled, table, dims, precision=highest, preferred_element...  9.48 us
    concatenate x1, other arithmetic, transform_table(): return jnp.concatenate([jnp.cos(angle), jnp.sin(angle)], axis=1)  8.16 us
    dot_general x1, matrix products, filter_units(): jnp.dot(flat, table, precision=highest, preferred_element_type=jnp.float32)  7.64 us
    ppermute x1, starting transfers between devices, padded_2(): lax.ppermute(tail, axis, [(i, (i + 1) % count) for i in range(ends)])  3.27 us
    slice x2, local copies, waits for them, and re-layouts, local(): west = jnp.roll(height, 1, axis=2)  2.85 us
    another operation x1, other arithmetic, local(): padded = padded_2(jnp.stack([height, merid_courant]), (('lat', 1),), 2)  2.78 us
  transfers between devices with their start and end apart: 2, of which 0 were waited for; matrix products, arithmetic and copies ran while one was open for 34% of the time, Pallas kernels for 0%

commit v1 on v0

--- a/solution.py
+++ b/solution.py
@@ -1,7 +1,15 @@
+import functools
 import jax
 import jax.numpy as jnp
 from jax import lax
 from jax.sharding import PartitionSpec as P
+
+
+def put_counts(slab_in, shard_axis):
+    return lax.all_gather(slab_in, shard_axis).sum(axis=0)
+
+
+register_the_sheets = functools.partial(put_counts, shard_axis="lat")
 
 
 def padded_2(cells, sides, width):
@@ -109,7 +117,7 @@
     zonal_div = zonal_flux - jnp.roll(zonal_flux, 1, axis=2)
     source = -rates[None, :, None] * jax.nn.softplus(height - thresholds[None, :, None])
     partial_sums = jnp.sum(jnp.sum(source, axis=2) * cos_rows[:, None], axis=0)
-    totals = lax.psum(partial_sums, "lat")
+    totals = register_the_sheets(partial_sums)
     all_rows = jnp.arange(nlat, dtype=jnp.int32)
     area = nlon * jnp.sum(jnp.sin(jnp.pi * (all_rows.astype(jnp.float32) + 0.5) / nlat))
     level_mean = totals / area

time: 102 us -> 105 us (1.029)
  other arithmetic: 36.4 us -> 38 us
  local copies, waits for them, and re-layouts: 5.82 us -> 6.91 us
    unnamed x0 -> x1, blocking collectives: none -> 35.8 us
    psum x1 -> x0, blocking collectives: 35.8 us -> none  [local(): totals = lax.psum(partial_sums, 'lat')]
    reduce_sum x2, other arithmetic: 1 us -> 2.59 us  [local(): partial_sums = jnp.sum(jnp.sum(source, axis=2) * cos_rows[:, None], axis=0)]
  transfers between devices with their start and end apart: 2 -> 2, of which waited for: 0 -> 0; matrix products, arithmetic and copies ran while one was open for 34% -> 36% of each run, Pallas kernels for 0% -> 0%
where the time goes in v1:
time: 105 us
  other arithmetic  38 us (36%)
  blocking collectives  35.8 us (34%)
  matrix products  17.1 us (16%)
  local copies, waits for them, and re-layouts  6.91 us (7%)
  starting transfers between devices  4.54 us (4%)
  between operations  2.04 us (2%)
    unnamed x1, blocking collectives  35.8 us
    sin x1, other arithmetic, transform_table(): return jnp.concatenate([jnp.cos(angle), jnp.sin(angle)], axis=1)  19.5 us
    dot_general x1, matrix products, filter_units(): lax.dot_general(scaled, table, dims, precision=highest, preferred_element...  9.48 us
    concatenate x1, other arithmetic, transform_table(): return jnp.concatenate([jnp.cos(angle), jnp.sin(angle)], axis=1)  8.16 us
    dot_general x1, matrix products, filter_units(): jnp.dot(flat, table, precision=highest, preferred_element_type=jnp.float32)  7.63 us
    ppermute x1, starting transfers between devices, padded_2(): lax.ppermute(tail, axis, [(i, (i + 1) % count) for i in range(ends)])  3.26 us
    slice x2, local copies, waits for them, and re-layouts, local(): west = jnp.roll(height, 1, axis=2)  2.97 us
    another operation x1, other arithmetic, local(): padded = padded_2(jnp.stack([height, merid_courant]), (('lat', 1),), 2)  2.77 us
  transfers between devices with their start and end apart: 2, of which 0 were waited for; matrix products, arithmetic and copies ran while one was open for 36% of the time, Pallas kernels for 0%

profile of v1, /device:TPU:0, one launch (start us, length us, event | category | flops | bytes accessed | tf_op | source)
XLA Modules:
  0.0 104.6 jit_solution(9163502437678456586)
XLA Ops:
  0.0 0.0 copy-start
  0.0 0.0 copy-start.2
  0.0 2.8 %fusion.17 = (f32[2,2,32,1440]{3,2,1,0:T(8,128)}, f32[2,2,32,1440]{3,2,1,0:T(8,128)}) fusion(f32[1,4,32,1440]{3,2,1,0:T(8,128)} %bitcast.22, f32[1,4,32,1440]{3,2,1,0:T(8,128)} %bitcast.28), kind=kLoop, calls=%fused_computation.33 | loop fusion | flops 368640 | bytes 2949120 | tf_op jit(solution)/shard_map/stack | solution.py:110
  2.8 3.3 %collective-permute-start = (f32[2,2,32,1440]{3,2,1,0:T(8,128)}, f32[2,2,32,1440]{3,2,1,0:T(8,128)}, u32[]{:S(2)}, u32[]{:S(2)}) collective-permute-start(f32[2,2,32,1440]{3,2,1,0:T(8,128)} %get-tuple-element.115), channel_id=1, source_target_pairs={{0,1},{1,2},{2,3},{3,4},{4,5},{5,6},{6,7},{7,8},{8,9},{9,10},{10,1... | collective-permute-start | bytes 2211848 | tf_op jit(solution)/shard_map/ppermute | solution.py:23
  6.0 1.3 %collective-permute-start.1 = (f32[2,2,32,1440]{3,2,1,0:T(8,128)}, f32[2,2,32,1440]{3,2,1,0:T(8,128)}, u32[]{:S(2)}, u32[]{:S(2)}) collective-permute-start(f32[2,2,32,1440]{3,2,1,0:T(8,128)} %get-tuple-element.116), channel_id=1, source_target_pairs={{1,0},{2,1},{3,2},{4,3},{5,4},{6,5},{7,6},{8,7},{9,8},{10,9},{11,1... | collective-permute-start | bytes 2211848 | tf_op jit(solution)/shard_map/ppermute | solution.py:25
  7.3 2.9 %fusion.33 = (f32[4,32,1439]{2,1,0:T(8,128)}, f32[4,32,1439]{2,1,0:T(8,128)}) fusion(f32[4,32,1440]{2,1,0:T(8,128)} %param.9), kind=kLoop, calls=%fused_computation.63 | loop fusion | bytes 2947072 | tf_op jit(solution)/shard_map/jit(_roll_static)/slice | solution.py:112
  10.2 0.0 copy-done
  10.2 0.1 fusion.32
  10.3 0.3 slice.95
  10.6 0.0 copy-done.2
  10.6 1.2 %slice.89 = f32[4,32,1439]{2,1,0:T(8,128)} slice(f32[4,32,1440]{2,1,0:T(8,128)S(1)} %copy-done.2), slice={[0:4], [0:32], [1:1440]} | slice | bytes 1473536 | tf_op jit(solution)/shard_map/jit(_roll_static)/slice | solution.py:115
  11.9 0.6 sine_reduce_fusion
  12.5 0.0 copy-start.7
  12.5 0.0 copy-start.3
  12.5 0.0 slice-start
  12.5 0.0 copy-start.5
  12.5 19.5 %fusion.7 = (f32[1440,768]{1,0:T(8,128)}, f32[1440,768]{1,0:T(8,128)}) fusion(), kind=kLoop, calls=%fused_computation.15 | loop fusion | flops 9953280 | bytes 8847360 | tf_op jit(solution)/shard_map/sin | solution.py:37
  32.1 0.0 copy-start.9
  32.1 0.0 copy-start.6
  32.1 0.0 copy-start.8
  32.1 0.0 copy-done.7
  32.1 0.0 copy-done.3
  32.1 0.0 slice-done
  32.1 0.0 copy-done.5
  32.1 2.5 %fusion.29 = (f32[4,32]{1,0:T(4,128)S(1)}, f32[4,32,1440]{2,1,0:T(8,128)S(1)}) fusion(f32[4,32,1440]{2,1,0:T(8,128)S(1)} %copy-done, f32[32]{0:T(128)S(1)} %copy-done.5, f32[32]{0:T(128)S(1)} %neg.8, f32[4,32,2]{2,1,0:T(8,128)S(1)} %slice.96, f32[4,32,1438]{2,1,0:T(8,128)S(1)} %slice.95, f32[4,32,1439]{2,1,0:T(8,128)} %get-tuple-element.121, ...), kind=kLoop, calls=%fused_computation.51 | loop fusion | flops 3870592 | bytes 5161728 | tf_op jit(solution)/shard_map/reduce_sum | solution.py:119
  34.7 0.1 multiply_reduce_fusion
  34.7 0.0 copy-done.9
  34.7 0.6 dynamic-slice
  36.0 0.2 dynamic-update-slice
  36.3 35.8 %all-reduce = f32[512]{0:T(512)S(1)} all-reduce(f32[512]{0:T(512)S(1)} %dynamic-update-slice), channel_id=2, replica_groups=mesh['member'=2,'lat'=16] {'lat'}, use_global_device_ids=true, to_apply=%add | all-reduce | flops 512 | bytes 4096
  72.1 0.1 reshape.117
  72.2 0.1 slice.109
  72.3 0.0 copy-done.6
  72.3 0.8 fusion.31
  73.0 0.0 copy-done.8
  73.0 0.1 dynamic-slice_convert_fusion
  74.3 0.0 copy-start.4
  74.3 8.2 %pad_maximum_fusion = f32[1440,1536]{1,0:T(8,128)} fusion(f32[1440,768]{1,0:T(8,128)} %get-tuple-element.123, f32[1440,768]{1,0:T(8,128)} %get-tuple-element.124), kind=kLoop, calls=%fused_computation.8 | loop fusion | flops 2211840 | bytes 17694720 | tf_op jit(solution)/shard_map/concatenate | solution.py:37
  82.5 0.0 collective-permute-done
  82.5 0.0 collective-permute-done.1
  82.5 0.0 copy-done.4
  82.5 1.9 %maximum_maximum_fusion = (f32[2,6,32,1440]{3,2,1,0:T(8,128)S(1)}, f32[2,6,32,1440]{3,2,1,0:T(8,128)S(1)}) fusion(f32[1,4,32,1440]{3,2,1,0:T(8,128)S(1)} %bitcast.29, f32[1,4,32,1440]{3,2,1,0:T(8,128)S(1)} %bitcast.23, f32[2,2,32,1440]{3,2,1,0:T(8,128)} %collective-permute-done, f32[2,2,32,1440]{3,2,1,0:T(8,128)} %collective-permute-done.1), kind=kLoop, calls=%fused_computation.18 | loop fusion | flops 2211840 | bytes 7372800 | tf_op jit(solution)/shard_map/concatenate | solution.py:21
  84.5 0.5 fusion.13
  85.0 0.7 fusion.22
  85.7 18.0 %conditional.1 = (f32[4,32,1440]{2,1,0:T(8,128)S(1)}) conditional(s32[]{:T(128)} %convert_element_type.42, f32[4,32,1440]{2,1,0:T(8,128)S(1)} %fusion.22, (f32[4,32,1440]{2,1,0:T(8,128)S(1)}, f32[1440,1536]{1,0:T(8,128)}, pred[4]{0:T(512)(128)(4,1)S(1)}, f32[4]{0:T(128)S(1)}, f32[1,768]{1,0:T(1,128)S(1)}, /*index=5*/s32[768]{0:T(1024)S(1)}) %tuple.45), branch_computations={%region_5.6_spmd, %region_6.7_spmd} | conditional | flops 6795468800 | bytes 25258016 | solution.py:80
  85.9 0.1 fusion.2
  86.1 7.6 %convolution_multiply_fusion = f32[128,1536]{1,0:T(8,128)S(1)} fusion(f32[128,1440]{1,0:T(8,128)S(1)} %bitcast.25, f32[1440,1536]{1,0:T(8,128)} %get-tuple-element.105, f32[128,768]{1,0:T(8,128)S(1)} %bitcast_multiply_fusion), kind=kOutput, calls=%fused_computation.1 | convolution fusion | flops 3397779456 | bytes 10764288 | tf_op jit(solution)/shard_map/cond/branch_1_fun/dot_general | solution.py:55
  93.7 0.3 copy.27
  94.0 9.5 %convolution_subtract_fusion = f32[128,1440]{0,1:T(8,128)S(1)} fusion(f32[128,1440]{0,1:T(8,128)S(1)} %copy.27, f32[128,1536]{1,0:T(8,128)S(1)} %convolution_multiply_fusion, f32[1440,1536]{1,0:T(8,128)} %get-tuple-element.105), kind=kOutput, calls=%fused_computation | convolution fusion | flops 3397570560 | bytes 11108352 | tf_op jit(solution)/shard_map/cond/branch_1_fun/dot_general | solution.py:59
  103.5 0.3 copy.28
  103.7 0.0 copy-start.1
  103.7 0.9 copy-done.1
  (12 shorter events, 0.2 us)
Async XLA Ops:
  0.0 10.2 %copy-start = (f32[4,32,1440]{2,1,0:T(8,128)S(1)}, f32[4,32,1440]{2,1,0:T(8,128)}, u32[]{:S(2)}) copy-start(f32[4,32,1440]{2,1,0:T(8,128)} %param.9) | copy-start | bytes 2211844
  0.0 10.6 %copy-start.2 = (f32[4,32,1440]{2,1,0:T(8,128)S(1)}, f32[4,32,1440]{2,1,0:T(8,128)}, u32[]{:S(2)}) copy-start(f32[4,32,1440]{2,1,0:T(8,128)} %param.10) | copy-start | bytes 2211844
  2.8 79.7 %collective-permute-start = (f32[2,2,32,1440]{3,2,1,0:T(8,128)}, f32[2,2,32,1440]{3,2,1,0:T(8,128)}, u32[]{:S(2)}, u32[]{:S(2)}) collective-permute-start(f32[2,2,32,1440]{3,2,1,0:T(8,128)} %get-tuple-element.115), channel_id=1, source_target_pairs={{0,1},{1,2},{2,3},{3,4},{4,5},{5,6},{6,7},{7,8},{8,9},{9,10},{10,1... | collective-permute-start | bytes 2211848 | tf_op jit(solution)/shard_map/ppermute | solution.py:23
  6.0 76.5 %collective-permute-start.1 = (f32[2,2,32,1440]{3,2,1,0:T(8,128)}, f32[2,2,32,1440]{3,2,1,0:T(8,128)}, u32[]{:S(2)}, u32[]{:S(2)}) collective-permute-start(f32[2,2,32,1440]{3,2,1,0:T(8,128)} %get-tuple-element.116), channel_id=1, source_target_pairs={{1,0},{2,1},{3,2},{4,3},{5,4},{6,5},{7,6},{8,7},{9,8},{10,9},{11,1... | collective-permute-start | bytes 2211848 | tf_op jit(solution)/shard_map/ppermute | solution.py:25
  12.5 19.6 %copy-start.7 = (f32[32]{0:T(128)S(1)}, f32[32]{0:T(128)}, u32[]{:S(2)}) copy-start(f32[32]{0:T(128)} %param.12) | copy-start | bytes 388
  12.5 19.6 %copy-start.3 = (f32[4,32,1440]{2,1,0:T(8,128)S(1)}, f32[4,32,1440]{2,1,0:T(8,128)}, u32[]{:S(2)}) copy-start(f32[4,32,1440]{2,1,0:T(8,128)} %param.10) | copy-start | bytes 2211844
  12.5 19.6 %slice-start = ((f32[4,32,1440]{2,1,0:T(8,128)}), f32[4,32,1]{2,1,0:T(8,128)S(1)}, s32[]{:S(2)}) async-start(f32[4,32,1440]{2,1,0:T(8,128)} %param.10), calls=%async_computation | async-start | bytes 131072 | tf_op jit(solution)/shard_map/jit(_roll_static)/slice | solution.py:115
  12.5 19.6 %copy-start.5 = (f32[32]{0:T(128)S(1)}, f32[32]{0:T(128)}, u32[]{:S(2)}) copy-start(f32[32]{0:T(128)} %param.13) | copy-start | bytes 388
  32.1 2.7 %copy-start.9 = (u32[32]{0:T(128)S(1)}, u32[32]{0:T(128)}, u32[]{:S(2)}) copy-start(u32[32]{0:T(128)} %constant.95) | copy-start | bytes 388
  32.1 40.2 %copy-start.6 = (s32[64]{0:T(128)S(1)}, s32[64]{0:T(128)}, u32[]{:S(2)}) copy-start(s32[64]{0:T(128)} %param.14) | copy-start | bytes 772
  32.1 41.0 %copy-start.8 = (s32[64]{0:T(128)S(1)}, s32[64]{0:T(128)}, u32[]{:S(2)}) copy-start(s32[64]{0:T(128)} %param.15) | copy-start | bytes 772
  74.3 8.2 %copy-start.4 = (f32[4,32,1440]{2,1,0:T(8,128)S(1)}, f32[4,32,1440]{2,1,0:T(8,128)}, u32[]{:S(2)}) copy-start(f32[4,32,1440]{2,1,0:T(8,128)} %param.11) | copy-start | bytes 2211844
  103.7 0.9 copy-start.1
